TPU v7x, 32 devices: a whole 2x2x4 slice. The times are simulated.
32 devices in a mesh: seq: 8 (over z, y), rep: 4 (over x, core).
Axes of the slice: x: 2, y: 2, z: 4, core: 2. Of those that a mesh axis runs over, the one named last changes fastest.
Arguments:
- query_rows: bfloat16 [12288, 1024], P(('seq', 'rep')), may hold values from -6 to 6
- key_rows: bfloat16 [12288, 128], P(('seq', 'rep')), may hold values from -6 to 6
- value_rows: bfloat16 [12288, 128], P(('seq', 'rep')), may hold values from -6 to 6
- out_grad: bfloat16 [12288, 1024], P(('seq', 'rep')), may hold values from -1.5 to 1.5
- logsumexp: float32 [8, 12288], P(None, ('seq', 'rep')), may hold values from 1 to 3
- row_delta: float32 [8, 12288], P(None, ('seq', 'rep')), may hold values from -8 to 8
- doc_lengths: int32 [31], replicated, may hold values from 1 to 1537, as said below
Outputs:
- query_grad: bfloat16 [12288, 1024], P(('seq', 'rep'))
- key_grad: bfloat16 [12288, 128], P(('seq', 'rep'))
- value_grad: bfloat16 [12288, 128], P(('seq', 'rep'))
Inputs may be any that keep to these rules, and one draw needn't show every extreme that they name: `doc_lengths`: 31 document lengths in pack order, summing to 12288; so every document lies within 5 consecutive aligned blocks of 384 positions.
All inputs are finite; a program needn't handle non-finite values.
Results may differ from a plain program's by a relative error of at most 0.019.
Values may be sent and summed in bfloat16 or wider, within the bound.
A program may use at most 64 MiB of HBM per device.

v0:
```python
import functools
import math

import jax
import jax.numpy as jnp
from jax import lax
from jax.experimental import pallas as pl
from jax.experimental.pallas import tpu as pltpu
from jax.sharding import PartitionSpec as P

REACH = 4
LANES = 128
UNROLL = 4
LOG2E = math.log2(math.e)
MESH = pl.DeviceIdType.MESH


def dot(a, b):
    return jnp.dot(a, b, preferred_element_type=jnp.float32)


def dot_nt(a, b):
    return lax.dot_general(a, b, (((1,), (1,)), ((), ())), preferred_element_type=jnp.float32)


def kernel(
    count,
    per_seq,
    lens_ref,
    q_hbm,
    g_hbm,
    k_ref,
    v_ref,
    lse_ref,
    delta_ref,
    dq_ref,
    dk_ref,
    dv_ref,
    q,
    g,
    kbuf,
    vbuf,
    k_t,
    bias,
    lse2,
    dq_t,
    own_k,
    own_v,
    acc_k,
    acc_v,
    out_k,
    out_v,
    in_k,
    in_v,
    load_sem,
    kv_send,
    kv_recv,
    gr_send,
    gr_recv,
):
    rows, head = k_ref.shape
    heads = q_hbm.shape[1] // head
    pack = 2 if heads % 2 == 0 else 1
    scale = head**-0.5
    me = lax.axis_index("seq") * per_seq + lax.axis_index("rep")

    def device(index):
        return (lax.div(index, per_seq), lax.rem(index, per_seq))

    loads = [
        pltpu.make_async_copy(
            src.at[:, h * head : (h + 1) * head],
            dst.at[h * rows : (h + 1) * rows, :],
            load_sem.at[n, h],
        )
        for h in range(heads)
        for n, (src, dst) in enumerate(((q_hbm, q), (g_hbm, g)))
    ]
    for copy in loads:
        copy.start()

    barrier = pltpu.get_barrier_semaphore()
    for d in range(1, REACH + 1):

        @pl.when(me + d < count)
        def _():
            pl.semaphore_signal(barrier, inc=1, device_id=device(me + d), device_id_type=MESH)

        @pl.when(me >= d)
        def _():
            pl.semaphore_signal(barrier, inc=1, device_id=device(me - d), device_id_type=MESH)

    pl.semaphore_wait(barrier, jnp.minimum(me, REACH) + jnp.minimum(count - 1 - me, REACH))

    core = lax.rem(me, 2)
    partner = me + 1 - 2 * core

    def kv_copies(sources, d, target, order):
        return [
            pltpu.make_async_remote_copy(
                src_ref=src,
                dst_ref=dst.at[d - 1],
                send_sem=kv_send.at[n, order],
                recv_sem=kv_recv.at[n, d - 1],
                device_id=device(target),
                device_id_type=MESH,
            )
            for n, (src, dst) in enumerate(zip(sources, (kbuf, vbuf)))
        ]

    own = (k_ref, v_ref)
    routes = [
        (me + 2 < count, kv_copies(own, 2, me + 2, 0)),
        (me + 4 < count, kv_copies(own, 4, me + 4, 1)),
        (core == 0, kv_copies(own, 1, partner, 2)),
        ((core == 0) & (me >= 2), kv_copies((kbuf.at[1], vbuf.at[1]), 3, partner, 3)),
        ((core == 1) & (me >= 2), kv_copies((kbuf.at[1], vbuf.at[1]), 1, partner, 3)),
        ((core == 1) & (me >= 4), kv_copies((kbuf.at[3], vbuf.at[3]), 3, partner, 4)),
    ]

    def send(numbers):
        for number in numbers:

            @pl.when(routes[number][0])
            def _():
                for copy in routes[number][1]:
                    copy.start()

    def grad_copies(d):
        return [
            pltpu.make_async_remote_copy(
                src_ref=src.at[d - 1],
                dst_ref=dst.at[d - 1],
                send_sem=gr_send.at[n, d - 1],
                recv_sem=gr_recv.at[n, d - 1],
                device_id=device(me - d),
                device_id_type=MESH,
            )
            for n, (src, dst) in enumerate(((out_k, in_k), (out_v, in_v)))
        ]

    send((0, 1, 2))

    t_pos = me * rows + lax.broadcasted_iota(jnp.int32, (1, rows), 1)

    def next_doc(j, carry):
        end, start = carry
        end = end + lens_ref[j]
        return end, jnp.where(end <= t_pos, end, start)

    _, start = lax.fori_loop(
        0, lens_ref.shape[0], next_doc, (jnp.int32(0), jnp.zeros((1, rows), jnp.int32))
    )
    lse2[...] = lse_ref[...] * LOG2E

    def set_bias(d):
        u_pos = (me - d) * rows + lax.broadcasted_iota(jnp.int32, (rows, rows), 0)
        bias[...] = jnp.where((u_pos >= start) & (u_pos <= t_pos), 0.0, -1e30)

    def columns(h):
        return pl.ds(pl.multiple_of(h * head, head), head)

    def stacked(h):
        return pl.ds(pl.multiple_of(h * rows, rows), pack * rows)

    def head_rows(ref, h):
        return jnp.concatenate([ref[pl.ds(h + n, 1), :] for n in range(pack)], axis=1)

    def grads(k_tile, v_tile, bias_tile, q_tile, g_tile, lse_tile, delta_tile):
        p = jnp.exp2(dot_nt(k_tile, q_tile) * (scale * LOG2E) + (bias_tile - lse_tile))
        ds = (p * (dot_nt(v_tile, g_tile) - delta_tile)).astype(jnp.bfloat16)
        return dot(ds, q_tile), dot(p.astype(jnp.bfloat16), g_tile), ds

    set_bias(0)
    k_t[...] = k_ref[...].astype(jnp.float32).T.astype(jnp.bfloat16)
    own_k[...] = jnp.zeros_like(own_k)
    own_v[...] = jnp.zeros_like(own_v)
    for copy in loads:
        copy.wait()
    tile = LANES if rows % LANES == 0 else rows

    def own_head(h, carry):
        dq_t[columns(h), :] = jnp.zeros((head, rows), jnp.float32)
        for low in range(0, rows, tile):
            u = slice(low, low + tile)
            t = pl.ds(pl.multiple_of(h * rows + low, tile), rows - low)
            dk, dv, ds = grads(
                k_ref[u, :],
                v_ref[u, :],
                bias[u, low:],
                q[t, :],
                g[t, :],
                lse2[pl.ds(h, 1), :][:, low:],
                delta_ref[pl.ds(h, 1), :][:, low:],
            )
            own_k[u, :] += dk
            own_v[u, :] += dv
            dq_t[columns(h), low:] += dot(k_t[:, u], ds)
        return carry

    lax.fori_loop(0, heads, own_head, 0, unroll=2)

    def cross(step, carry):
        d = 2 * (step + 1) - lax.div(step, 2) * (4 * step - 5)

        @pl.when(me >= d)
        def _():
            for copy in kv_copies(own, d, partner, 0):
                copy.wait_recv()

            @pl.when(step == 0)
            def _():
                send((3, 4))

            @pl.when(step == 1)
            def _():
                send((5,))

            set_bias(d)
            k_t[...] = kbuf[d - 1].astype(jnp.float32).T.astype(jnp.bfloat16)
            acc_k[...] = jnp.zeros_like(acc_k)
            acc_v[...] = jnp.zeros_like(acc_v)

            def one_pack(n, inner):
                h = n * pack
                dk, dv, ds = grads(
                    kbuf[d - 1],
                    vbuf[d - 1],
                    jnp.concatenate([bias[...]] * pack, axis=1),
                    q[stacked(h), :],
                    g[stacked(h), :],
                    head_rows(lse2, h),
                    head_rows(delta_ref, h),
                )
                acc_k[...] += dk
                acc_v[...] += dv
                dq = dot(k_t[...], ds)
                for m in range(pack):
                    dq_t[columns(h + m), :] += dq[:, m * rows : (m + 1) * rows]
                return inner

            lax.fori_loop(0, heads // pack, one_pack, 0, unroll=UNROLL)
            out_k[d - 1] = (acc_k[...] * scale).astype(jnp.bfloat16)
            out_v[d - 1] = acc_v[...].astype(jnp.bfloat16)
            for copy in grad_copies(d):
                copy.start()

        return carry

    lax.fori_loop(0, REACH, cross, 0)

    for h in range(heads):
        c = slice(h * head, (h + 1) * head)
        dq_ref[:, c] = (dq_t[c, :] * scale).T.astype(jnp.bfloat16)

    own_k[...] = own_k[...] * scale
    for used, copies in routes:

        @pl.when(used)
        def _():
            for copy in copies:
                copy.wait_send()

    for d in (2, 4, 3, 1):

        @pl.when(me + d < count)
        def _():
            for copy in grad_copies(d):
                copy.wait_recv()
            own_k[...] += in_k[d - 1].astype(jnp.float32)
            own_v[...] += in_v[d - 1].astype(jnp.float32)
        @pl.when(me >= d)
        def _():
            for copy in grad_copies(d):
                copy.wait_send()

    dk_ref[...] = own_k[...].astype(jnp.bfloat16)
    dv_ref[...] = own_v[...].astype(jnp.bfloat16)


def pass_on(dq_ref, dk_ref, dv_ref, dq_out, dk_out, dv_out):
    dq_out[...] = dq_ref[...]
    dk_out[...] = dk_ref[...]
    dv_out[...] = dv_ref[...]


def shards(count, per_seq, query_rows, key_rows, value_rows, out_grad, logsumexp, row_delta, doc_lengths):
    rows, head = key_rows.shape
    wide = query_rows.shape
    heads = wide[1] // head
    half, full = jnp.bfloat16, jnp.float32
    vmem = pl.BlockSpec(memory_space=pltpu.VMEM)
    hbm = pl.BlockSpec(memory_space=pl.ANY)
    grads = pl.pallas_call(
        functools.partial(kernel, count, per_seq),
        out_shape=(
            jax.ShapeDtypeStruct(wide, half),
            jax.ShapeDtypeStruct((rows, head), half),
            jax.ShapeDtypeStruct((rows, head), half),
        ),
        in_specs=[pl.BlockSpec(memory_space=pltpu.SMEM), hbm, hbm, vmem, vmem, vmem, vmem],
        out_specs=(vmem, vmem, vmem),
        scratch_shapes=[
            pltpu.VMEM((heads * rows, head), half),
            pltpu.VMEM((heads * rows, head), half),
            pltpu.VMEM((REACH, rows, head), half),
            pltpu.VMEM((REACH, rows, head), half),
            pltpu.VMEM((head, rows), half),
            pltpu.VMEM((rows, rows), full),
            pltpu.VMEM(logsumexp.shape, full),
            pltpu.VMEM((wide[1], rows), full),
            pltpu.VMEM((rows, head), full),
            pltpu.VMEM((rows, head), full),
            pltpu.VMEM((rows, head), full),
            pltpu.VMEM((rows, head), full),
            pltpu.VMEM((REACH, rows, head), half),
            pltpu.VMEM((REACH, rows, head), half),
            pltpu.VMEM((REACH, rows, head), half),
            pltpu.VMEM((REACH, rows, head), half),
            pltpu.SemaphoreType.DMA((2, heads)),
            pltpu.SemaphoreType.DMA((2, 5)),
            pltpu.SemaphoreType.DMA((2, REACH)),
            pltpu.SemaphoreType.DMA((2, REACH)),
            pltpu.SemaphoreType.DMA((2, REACH)),
        ],
        compiler_params=pltpu.CompilerParams(collective_id=0, has_side_effects=True),
    )(doc_lengths, query_rows, out_grad, key_rows, value_rows, logsumexp, row_delta)
    return pl.pallas_call(
        pass_on,
        out_shape=tuple(jax.ShapeDtypeStruct(part.shape, part.dtype) for part in grads),
        in_specs=[vmem] * 3,
        out_specs=(vmem,) * 3,
    )(*grads)


def solution(mesh):
    both = ("seq", "rep")
    count = mesh.shape["seq"] * mesh.shape["rep"]
    return jax.shard_map(
        functools.partial(shards, count, mesh.shape["rep"]),
        mesh=mesh,
        in_specs=(
            P(both, None),
            P(both, None),
            P(both, None),
            P(both, None),
            P(None, both),
            P(None, both),
            P(),
        ),
        out_specs=(P(both, None), P(both, None), P(both, None)),
        check_vma=False,
    )
```

profile of v0, /device:TPU:7, one launch (start us, length us, event | category | flops | bytes accessed | tf_op | source)
XLA Modules:
  0.0 36.9 jit_solution(6741091907764791452)
XLA Ops:
  0.6 34.1 %shard_map.94 = (bf16[384,1024]{1,0:T(8,128)(2,1)}, bf16[384,128]{1,0:T(8,128)(2,1)}, bf16[384,128]{1,0:T(8,128)(2,1)}) custom-call(s32[31]{0:T(128)} %lens_ref.1, bf16[384,1024]{1,0:T(8,128)(2,1)} %q_hbm.1, bf16[384,1024]{1,0:T(8,128)(2,1)} %g_hbm.1, bf16[384,128]{1,0:T(8,128)(2,1)} %k_ref.1, bf16[384,128]{1,0:T(8,128)(2,1)} %v_ref.1, f32[8,384]{1,0:T(8,128)} %lse_ref.1, ...), custom_call_target="tpu_custom_call" | custom-call | tf_op jit(solution)/shard_map/pallas_call | solution.py:294
  34.7 2.2 %shard_map.95 = (bf16[384,1024]{1,0:T(8,128)(2,1)}, bf16[384,128]{1,0:T(8,128)(2,1)}, bf16[384,128]{1,0:T(8,128)(2,1)}) custom-call(bf16[384,1024]{1,0:T(8,128)(2,1)} %get-tuple-element.6.dq_ref, bf16[384,128]{1,0:T(8,128)(2,1)} %get-tuple-element.7.dk_ref, bf16[384,128]{1,0:T(8,128)(2,1)} %get-tuple-element.8.dv_ref), custom_call_target="tpu_custom_call" | custom-call | tf_op jit(solution)/shard_map/pallas_call | solution.py:328
where the time goes:
time: 37.1 us; the launch traced here: 36.9 us
  Pallas kernels  36.3 us (98%)
  between operations  0.64 us (2%)
    pallas_call x1, Pallas kernels, shards(): pl.pallas_call(functools.partial(kernel, count, per_seq), out_shape=(jax....  34.1 us
    pallas_call x1, Pallas kernels, shards(): pl.pallas_call(pass_on, out_shape=tuple((jax.ShapeDtypeStruct(part.shape,...  2.15 us

commit v1 on v0

v1 whole, which is shorter than its diff:
```python
import functools
import math

import jax
import jax.numpy as jnp
from jax import lax
from jax.experimental import pallas as pl
from jax.experimental.pallas import tpu as pltpu
from jax.sharding import PartitionSpec as P

REACH = 4
LANES = 128
LOG2E = math.log2(math.e)
MESH = pl.DeviceIdType.MESH
MIB = 1024 * 1024


def dot(a, b):
    return jnp.dot(a, b, preferred_element_type=jnp.float32)


def dot_nt(a, b):
    return lax.dot_general(a, b, (((1,), (1,)), ((), ())), preferred_element_type=jnp.float32)


def turned(a):
    return a.astype(jnp.float32).T.astype(jnp.bfloat16)


def kernel(
    count,
    per_seq,
    lens_hbm,
    q_hbm,
    g_hbm,
    k_hbm,
    v_hbm,
    lse_hbm,
    delta_hbm,
    dq_ref,
    dk_ref,
    dv_ref,
    lens,
    q,
    g,
    qt,
    gt,
    own,
    kv,
    k_t,
    bias,
    lse,
    delta,
    lse_row,
    delta_row,
    dq_t,
    own_acc,
    acc,
    out,
    part,
    ret,
    load_sem,
    small_sem,
    kv_send,
    kv_recv,
    part_send,
    part_recv,
    ret_send,
    ret_recv,
):
    rows, head = k_hbm.shape
    heads = q_hbm.shape[1] // head
    pack = 2 if heads % 2 == 0 else 1
    tile = LANES if rows % LANES == 0 else rows
    wide = rows // (2 * tile) * (2 * tile)
    scale = head**-0.5
    me = lax.axis_index("seq") * per_seq + lax.axis_index("rep")
    core = lax.rem(me, 2)
    partner = me + 1 - 2 * core

    def device(index):
        return (lax.div(index, per_seq), lax.rem(index, per_seq))

    def when(*conditions):
        return pl.when(functools.reduce(jnp.logical_and, conditions))

    barrier = pltpu.get_barrier_semaphore()

    def greet(target):
        pl.semaphore_signal(barrier, inc=1, device_id=device(target), device_id_type=MESH)

    greet(partner)
    for d in (2, 4):
        pl.when(me + d < count)(functools.partial(greet, me + d))
        pl.when(me >= d)(functools.partial(greet, me - d))

    small = [
        pltpu.make_async_copy(src, dst, small_sem.at[n])
        for n, (src, dst) in enumerate(
            (
                (lens_hbm, lens),
                (k_hbm, own.at[0]),
                (v_hbm, own.at[1]),
                (lse_hbm, lse),
                (delta_hbm, delta),
            )
        )
    ]
    loads = [
        [
            pltpu.make_async_copy(
                src.at[:, h * head : (h + 1) * head],
                dst.at[h * rows : (h + 1) * rows, :],
                load_sem.at[n, h],
            )
            for n, (src, dst) in enumerate(((q_hbm, q), (g_hbm, g)))
        ]
        for h in range(heads)
    ]
    for copy in small:
        copy.start()
    for pair in loads:
        for copy in pair:
            copy.start()

    def remote(src, dst, send_sem, recv_sem, target):
        return pltpu.make_async_remote_copy(
            src_ref=src,
            dst_ref=dst,
            send_sem=send_sem,
            recv_sem=recv_sem,
            device_id=device(target),
            device_id_type=MESH,
        )

    def kv_copy(src, slot, order, target):
        return remote(src, kv.at[slot], kv_send.at[order], kv_recv.at[slot], target)

    def part_copy(step, slot):
        return remote(out.at[step], part.at[slot], part_send.at[slot], part_recv.at[slot], partner)

    def ret_copy(step, d):
        n = d // 2 - 1
        return remote(out.at[step], ret.at[n], ret_send.at[n], ret_recv.at[n], me - d)

    send_partner = kv_copy(own, 0, 2, partner)
    send_near = kv_copy(own, 3 * core, 0, me + 2)
    send_far = kv_copy(own, 3 - core, 1, me + 4)

    for copy in small[1:3]:
        copy.wait()
    pl.semaphore_wait(
        barrier,
        1 + jnp.minimum(me, REACH) // 2 + jnp.minimum(count - 1 - me, REACH) // 2,
    )

    @when(core == 0)
    def _():
        send_partner.start()

    @when(core == 1, me + 4 < count)
    def _():
        send_far.start()

    @when(me + 2 < count)
    def _():
        send_near.start()

    @when(core == 0, me + 4 < count)
    def _():
        send_far.start()

    small[0].wait()
    t_pos = me * rows + lax.broadcasted_iota(jnp.int32, (1, rows), 1)
    docs = lens.shape[1]
    upto = lax.broadcasted_iota(jnp.int32, (docs, docs), 1) <= lax.broadcasted_iota(
        jnp.int32, (docs, docs), 0
    )
    ends = jnp.sum(jnp.where(upto, lens[...].astype(jnp.float32), 0.0), axis=1, keepdims=True)
    begun = jnp.where(ends <= t_pos.astype(jnp.float32), ends, 0.0)
    start = jnp.max(begun, axis=0, keepdims=True).astype(jnp.int32)
    for copy in small[3:]:
        copy.wait()
    for h in range(heads):
        c = slice(h * rows, (h + 1) * rows)
        lse_row[:, c] = lse[h : h + 1, :] * LOG2E
        delta_row[:, c] = delta[h : h + 1, :]

    def set_bias(d):
        u_pos = (me - d) * rows + lax.broadcasted_iota(jnp.int32, (rows, rows), 0)
        bias[...] = jnp.where((u_pos >= start) & (u_pos <= t_pos), 0.0, -1e30)

    def stack(ref, pieces):
        return jnp.concatenate([ref[h * rows + t : h * rows + t + n, :] for h, t, n in pieces], axis=0)

    def line(ref, pieces):
        return jnp.concatenate([ref[:, h * rows + t : h * rows + t + n] for h, t, n in pieces], axis=1)

    def put(ref, index, value, fresh):
        ref[index] = value if fresh else ref[index] + value

    def scores(k_ref, v_ref, item):
        pieces, low, high = item
        u = slice(low, high)
        return dot_nt(k_ref[u, :], stack(q, pieces)), dot_nt(v_ref[u, :], stack(g, pieces))

    def finish(item, s, dp, acc_ref, seen, first_dq):
        pieces, low, high = item
        u = slice(low, high)
        mask = jnp.concatenate([bias[u, t : t + n] for _, t, n in pieces], axis=1)
        p = jnp.exp2(s * (scale * LOG2E) + (mask - line(lse_row, pieces)))
        ds = (p * (dp - line(delta_row, pieces))).astype(jnp.bfloat16)
        p = p.astype(jnp.bfloat16)
        for n, (weight, turned_rows, plain_rows) in enumerate(((ds, qt, q), (p, gt, g))):
            if low < wide:
                top = min(high, wide)
                part_t = dot_nt(line(turned_rows, pieces), weight[: top - low, :])
                for i in range(low // tile, top // tile):
                    at = i * tile - low
                    put(acc_ref, (n, i), part_t[:, at : at + tile], (n, i) not in seen)
                    seen.add((n, i))
            if high > wide:
                base = max(low, wide)
                part_n = dot(weight[base - low :, :], stack(plain_rows, pieces))
                for i in range(base // tile, high // tile):
                    at = i * tile - base
                    put(acc_ref, (n, i), part_n[at : at + tile, :], (n, i) not in seen)
                    seen.add((n, i))
        dq = dot(k_t[:, u], ds)
        at = 0
        for h, t, n in pieces:
            put(dq_t, (slice(None), slice(h * rows + t, h * rows + t + n)), dq[:, at : at + n], first_dq)
            at += n

    def sweep(k_ref, v_ref, items, acc_ref, first_dq, before=None):
        seen = set()
        held = None
        for n, item in enumerate(items):
            if before is not None:
                before(n)
            ahead = scores(k_ref, v_ref, item)
            if held is not None:
                finish(*held, acc_ref, seen, first_dq)
            held = (item, *ahead)
        finish(*held, acc_ref, seen, first_dq)

    def runs(begin, width):
        pieces = []
        while width:
            t = begin % rows
            n = min(width, rows - t)
            pieces.append((begin // rows, t, n))
            begin, width = begin + n, width - n
        return pieces

    span = 2 * tile
    full_items = [(runs(b, span), 0, rows) for b in range(0, heads * rows, span)]
    pairs = [[h + m for m in range(pack)] for h in range(0, heads, pack)]
    own_items = [
        ([(h, t, tile) for h in pair], 0, t + tile) for pair in pairs for t in reversed(range(0, rows, tile))
    ]
    far_items = [([(h, t, tile) for h in pair], t, rows) for pair in pairs for t in range(0, rows, tile)]

    set_bias(0)
    k_t[...] = turned(own[0])

    def bring(n):
        if n % (rows // tile) == 0:
            for h in pairs[n // (rows // tile)]:
                for copy in loads[h]:
                    copy.wait()
                c = slice(h * rows, (h + 1) * rows)
                qt[:, c] = turned(q[c, :])
                gt[:, c] = turned(g[c, :])

    sweep(own.at[0], own.at[1], own_items, own_acc, True, bring)

    def round_out(step):
        out[step] = acc[step].astype(jnp.bfloat16)

    def merge_out(step, slot, d):
        part_copy(step, slot).wait_recv()
        out[step] = (acc[step] + part[slot].astype(jnp.float32)).astype(jnp.bfloat16)
        ret_copy(step, d).start()

    def arrive(slot):
        kv_copy(own, slot, 0, partner).wait_recv()

    def step_body(step, carry):
        even = step + 2 - lax.div(step, 2) * (7 - 2 * step)
        odd = 2 * step + 1 - lax.div(step, 2) * (4 * step - 7)
        d = even + core * (odd - even)

        @when(core == 0, me >= d)
        def _():
            arrive(step)

        @when(core == 0, step == 0, me >= 2)
        def _():
            kv_copy(kv.at[0], 1, 3, partner).start()

        @when(core == 1, step == 0)
        def _():
            arrive(0)

        @when(core == 1, step == 1, me >= 4)
        def _():
            arrive(2)
            kv_copy(kv.at[2], 1, 4, partner).start()

        @when(core == 1, step == 1, me >= 3)
        def _():
            arrive(1)

        @when(core == 1, step == 2, me >= 2)
        def _():
            arrive(3)
            kv_copy(kv.at[3], 2, 3, partner).start()

        @when(me >= d)
        def _():
            set_bias(d)
            k_t[...] = turned(kv[step, 0])

            @when(d == REACH)
            def _():
                sweep(kv.at[step, 0], kv.at[step, 1], far_items, acc.at[step], False)

            @when(d != REACH)
            def _():
                sweep(kv.at[step, 0], kv.at[step, 1], full_items, acc.at[step], False)

        @when(core == 0, step == 1, me >= 3)
        def _():
            round_out(1)
            part_copy(1, 1).start()

        @when(core == 0, step == 1, me >= 2)
        def _():
            merge_out(0, 0, 2)

        @when(core == 0, step == 2, me >= 1)
        def _():
            round_out(2)
            part_copy(2, 0).start()

        @when(core == 0, step == 3, me >= 4)
        def _():
            round_out(3)
            ret_copy(3, 4).start()

        @when(core == 1, step == 0)
        def _():
            round_out(0)
            part_copy(0, 1).start()

        @when(core == 1, step == 1, me >= 3)
        def _():
            round_out(1)
            part_copy(1, 0).start()

        @when(core == 1, step == 3, me >= 4)
        def _():
            merge_out(2, 1, 4)

        @when(core == 1, step == 3, me >= 2)
        def _():
            merge_out(3, 0, 2)

        return carry

    lax.fori_loop(0, REACH, step_body, 0)

    for h in range(heads):
        c = slice(h * head, (h + 1) * head)
        dq_ref[:, c] = (dq_t[:, h * rows : (h + 1) * rows] * scale).T.astype(jnp.bfloat16)

    @when(core == 0)
    def _():
        part_copy(1, 1).wait_recv()
        own_acc[...] = own_acc[...] + part[1].astype(jnp.float32)

    for d in (2, 4):

        @when(me + d < count)
        def _():
            ret_copy(0, d).wait_recv()
            own_acc[...] = own_acc[...] + ret[d // 2 - 1].astype(jnp.float32)

    for i in range(rows // tile):
        r = slice(i * tile, (i + 1) * tile)
        dk = own_acc[0, i] * scale
        dv = own_acc[1, i]
        dk_ref[r, :] = (dk.T if i * tile < wide else dk).astype(jnp.bfloat16)
        dv_ref[r, :] = (dv.T if i * tile < wide else dv).astype(jnp.bfloat16)

    @when(me + 2 < count)
    def _():
        send_near.wait_send()

    @when(me + 4 < count)
    def _():
        send_far.wait_send()

    @when(core == 0)
    def _():
        send_partner.wait_send()

    @when(me >= 2)
    def _():
        kv_copy(kv.at[0], 1, 3, partner).wait_send()
        part_copy(0, 0).wait_send()
        ret_copy(0, 2).wait_send()

    @when(me >= 4)
    def _():
        ret_copy(0, 4).wait_send()

    @when(core == 1, me >= 4)
    def _():
        kv_copy(kv.at[2], 1, 4, partner).wait_send()

    @when((core == 1) | (me >= 4))
    def _():
        part_copy(0, 1).wait_send()


def pass_on(dq_ref, dk_ref, dv_ref, dq_out, dk_out, dv_out, sem):
    copies = [
        pltpu.make_async_copy(src, dst, sem.at[n])
        for n, (src, dst) in enumerate(((dq_ref, dq_out), (dk_ref, dk_out), (dv_ref, dv_out)))
    ]
    for copy in copies:
        copy.start()
    for copy in copies:
        copy.wait()


def shards(count, per_seq, query_rows, key_rows, value_rows, out_grad, logsumexp, row_delta, doc_lengths):
    rows, head = key_rows.shape
    wide = query_rows.shape
    heads = wide[1] // head
    sums = (2, rows // LANES, LANES, head)
    half, full = jnp.bfloat16, jnp.float32
    vmem = pl.BlockSpec(memory_space=pltpu.VMEM)
    hbm = pl.BlockSpec(memory_space=pl.ANY)
    operands = [
        pltpu.with_memory_space_constraint(x, pltpu.HBM)
        for x in (doc_lengths.reshape(1, -1), query_rows, out_grad, key_rows, value_rows, logsumexp, row_delta)
    ]
    grads = pl.pallas_call(
        functools.partial(kernel, count, per_seq),
        out_shape=(
            jax.ShapeDtypeStruct(wide, half),
            jax.ShapeDtypeStruct((rows, head), half),
            jax.ShapeDtypeStruct((rows, head), half),
        ),
        in_specs=[hbm] * 7,
        out_specs=(vmem, vmem, vmem),
        scratch_shapes=[
            pltpu.VMEM((1, doc_lengths.shape[0]), jnp.int32),
            pltpu.VMEM((heads * rows, head), half),
            pltpu.VMEM((heads * rows, head), half),
            pltpu.VMEM((head, heads * rows), half),
            pltpu.VMEM((head, heads * rows), half),
            pltpu.VMEM((2, rows, head), half),
            pltpu.VMEM((REACH, 2, rows, head), half),
            pltpu.VMEM((head, rows), half),
            pltpu.VMEM((rows, rows), full),
            pltpu.VMEM(logsumexp.shape, full),
            pltpu.VMEM(row_delta.shape, full),
            pltpu.VMEM((1, heads * rows), full),
            pltpu.VMEM((1, heads * rows), full),
            pltpu.VMEM((head, heads * rows), full),
            pltpu.VMEM(sums, full),
            pltpu.VMEM((REACH, *sums), full),
            pltpu.VMEM((REACH, *sums), half),
            pltpu.VMEM((2, *sums), half),
            pltpu.VMEM((2, *sums), half),
            pltpu.SemaphoreType.DMA((2, heads)),
            pltpu.SemaphoreType.DMA((5,)),
            pltpu.SemaphoreType.DMA((5,)),
            pltpu.SemaphoreType.DMA((REACH,)),
            pltpu.SemaphoreType.DMA((2,)),
            pltpu.SemaphoreType.DMA((2,)),
            pltpu.SemaphoreType.DMA((2,)),
            pltpu.SemaphoreType.DMA((2,)),
        ],
        compiler_params=pltpu.CompilerParams(
            collective_id=0, has_side_effects=True, vmem_limit_bytes=40 * MIB
        ),
    )(*operands)
    return pl.pallas_call(
        pass_on,
        out_shape=tuple(jax.ShapeDtypeStruct(x.shape, x.dtype) for x in grads),
        in_specs=[vmem] * 3,
        out_specs=(hbm,) * 3,
        scratch_shapes=[pltpu.SemaphoreType.DMA((3,))],
        compiler_params=pltpu.CompilerParams(vmem_limit_bytes=8 * MIB),
    )(*grads)


def solution(mesh):
    both = ("seq", "rep")
    count = mesh.shape["seq"] * mesh.shape["rep"]
    return jax.shard_map(
        functools.partial(shards, count, mesh.shape["rep"]),
        mesh=mesh,
        in_specs=(
            P(both, None),
            P(both, None),
            P(both, None),
            P(both, None),
            P(None, both),
            P(None, both),
            P(),
        ),
        out_specs=(P(both, None), P(both, None), P(both, None)),
        check_vma=False,
    )
```

time: 37.1 us -> 32 us (0.86)
  the two profiles are of different devices: /device:TPU:7 before, /device:TPU:4 now
where the time goes in v1:
time: 32 us; the launch traced here: 31.8 us
  Pallas kernels  31.2 us (98%)
  between operations  0.64 us (2%)
    pallas_call x1, Pallas kernels, shards(): pl.pallas_call(functools.partial(kernel, count, per_seq), out_shape=(jax....  30.2 us
    pallas_call x1, Pallas kernels, shards(): pl.pallas_call(pass_on, out_shape=tuple((jax.ShapeDtypeStruct(x.shape, x....  0.96 us

profile of v1, /device:TPU:4, one launch (start us, length us, event | category | flops | bytes accessed | tf_op | source)
XLA Modules:
  0.0 31.8 jit_solution(5059837062160399622)
XLA Ops:
  0.6 30.2 %shard_map.94 = (bf16[384,1024]{1,0:T(8,128)(2,1)S(1)}, bf16[384,128]{1,0:T(8,128)(2,1)S(1)}, bf16[384,128]{1,0:T(8,128)(2,1)S(1)}) custom-call(s32[1,31]{1,0:T(1,128)} %bitcast.1, bf16[384,1024]{1,0:T(8,128)(2,1)} %q_hbm.1, bf16[384,1024]{1,0:T(8,128)(2,1)} %g_hbm.1, bf16[384,128]{1,0:T(8,128)(2,1)} %k_hbm.1, bf16[384,128]{1,0:T(8,128)(2,1)} %v_hbm.1, ...), custom_call_target="tpu_custom_call" | custom-call | tf_op jit(solution)/shard_map/pallas_call | solution.py:451
  30.8 1.0 %shard_map.95 = (bf16[384,1024]{1,0:T(8,128)(2,1)}, bf16[384,128]{1,0:T(8,128)(2,1)}, bf16[384,128]{1,0:T(8,128)(2,1)}) custom-call(bf16[384,1024]{1,0:T(8,128)(2,1)S(1)} %get-tuple-element.6.dq_ref, bf16[384,128]{1,0:T(8,128)(2,1)S(1)} %get-tuple-element.7.dk_ref, bf16[384,128]{1,0:T(8,128)(2,1)S(1)} %get-tuple-element.8.dv_ref), custom_call_target="tpu_custom_call" | custom-call | tf_op jit(solution)/shard_map/pallas_call | solution.py:493

commit v2 on v1

--- a/solution.py
+++ b/solution.py
@@ -84,23 +84,13 @@
     def when(*conditions):
         return pl.when(functools.reduce(jnp.logical_and, conditions))
 
-    barrier = pltpu.get_barrier_semaphore()
-
-    def greet(target):
-        pl.semaphore_signal(barrier, inc=1, device_id=device(target), device_id_type=MESH)
-
-    greet(partner)
-    for d in (2, 4):
-        pl.when(me + d < count)(functools.partial(greet, me + d))
-        pl.when(me >= d)(functools.partial(greet, me - d))
-
     small = [
         pltpu.make_async_copy(src, dst, small_sem.at[n])
         for n, (src, dst) in enumerate(
             (
-                (lens_hbm, lens),
                 (k_hbm, own.at[0]),
                 (v_hbm, own.at[1]),
+                (lens_hbm, lens),
                 (lse_hbm, lse),
                 (delta_hbm, delta),
             )
@@ -119,9 +109,16 @@
     ]
     for copy in small:
         copy.start()
-    for pair in loads:
-        for copy in pair:
-            copy.start()
+
+    barrier = pltpu.get_barrier_semaphore()
+
+    def greet(target):
+        pl.semaphore_signal(barrier, inc=1, device_id=device(target), device_id_type=MESH)
+
+    greet(partner)
+    for d in (2, 4):
+        pl.when(me + d < count)(functools.partial(greet, me + d))
+        pl.when(me >= d)(functools.partial(greet, me - d))
 
     def remote(src, dst, send_sem, recv_sem, target):
         return pltpu.make_async_remote_copy(
@@ -147,8 +144,11 @@
     send_near = kv_copy(own, 3 * core, 0, me + 2)
     send_far = kv_copy(own, 3 - core, 1, me + 4)
 
-    for copy in small[1:3]:
+    for copy in small[:2]:
         copy.wait()
+    for pair in loads:
+        for copy in pair:
+            copy.start()
     pl.semaphore_wait(
         barrier,
         1 + jnp.minimum(me, REACH) // 2 + jnp.minimum(count - 1 - me, REACH) // 2,
@@ -158,19 +158,11 @@
     def _():
         send_partner.start()
 
-    @when(core == 1, me + 4 < count)
-    def _():
-        send_far.start()
-
-    @when(me + 2 < count)
+    @when(core == 0, me + 2 < count)
     def _():
         send_near.start()
 
-    @when(core == 0, me + 4 < count)
-    def _():
-        send_far.start()
-
-    small[0].wait()
+    small[2].wait()
     t_pos = me * rows + lax.broadcasted_iota(jnp.int32, (1, rows), 1)
     docs = lens.shape[1]
     upto = lax.broadcasted_iota(jnp.int32, (docs, docs), 1) <= lax.broadcasted_iota(
@@ -275,6 +267,10 @@
 
     sweep(own.at[0], own.at[1], own_items, own_acc, True, bring)
 
+    @when(core == 1, me + 4 < count)
+    def _():
+        send_far.start()
+
     def round_out(step):
         out[step] = acc[step].astype(jnp.bfloat16)
 
@@ -330,7 +326,15 @@
             def _():
                 sweep(kv.at[step, 0], kv.at[step, 1], full_items, acc.at[step], False)
 
-        @when(core == 0, step == 1, me >= 3)
+        @when(core == 1, step == 0, me + 2 < count)
+        def _():
+            send_near.start()
+
+        @when(core == 0, step == 0, me + 4 < count)
+        def _():
+            send_far.start()
+
+        @when(core == 0, step == 1, me >= 4)
         def _():
             round_out(1)
             part_copy(1, 1).start()
@@ -339,7 +343,7 @@
         def _():
             merge_out(0, 0, 2)
 
-        @when(core == 0, step == 2, me >= 1)
+        @when(core == 0, step == 2, me >= 2)
         def _():
             round_out(2)
             part_copy(2, 0).start()
@@ -359,7 +363,7 @@
             round_out(1)
             part_copy(1, 0).start()
 
-        @when(core == 1, step == 3, me >= 4)
+        @when(core == 1, step == 2, me >= 4)
         def _():
             merge_out(2, 1, 4)
 

time: 32 us -> 29.4 us (0.919)
  Pallas kernels: 31.2 us -> 28.5 us
    pallas_call x1, Pallas kernels: 30.2 us -> 27.6 us  [shards(): pl.pallas_call(functools.partial(kernel, count, per_seq), out_shape=(jax....]
where the time goes in v2:
time: 29.4 us; the launch traced here: 29.2 us
  Pallas kernels  28.5 us (97%)
  between operations  0.64 us (2%)
    pallas_call x1, Pallas kernels, shards(): pl.pallas_call(functools.partial(kernel, count, per_seq), out_shape=(jax....  27.6 us
    pallas_call x1, Pallas kernels, shards(): pl.pallas_call(pass_on, out_shape=tuple((jax.ShapeDtypeStruct(x.shape, x....  0.96 us

profile of v2, /device:TPU:4, one launch (start us, length us, event | category | flops | bytes accessed | tf_op | source)
XLA Modules:
  0.0 29.2 jit_solution(6348153008631127903)
XLA Ops:
  0.6 27.6 %shard_map.94 = (bf16[384,1024]{1,0:T(8,128)(2,1)S(1)}, bf16[384,128]{1,0:T(8,128)(2,1)S(1)}, bf16[384,128]{1,0:T(8,128)(2,1)S(1)}) custom-call(s32[1,31]{1,0:T(1,128)} %bitcast.1, bf16[384,1024]{1,0:T(8,128)(2,1)} %q_hbm.1, bf16[384,1024]{1,0:T(8,128)(2,1)} %g_hbm.1, bf16[384,128]{1,0:T(8,128)(2,1)} %k_hbm.1, bf16[384,128]{1,0:T(8,128)(2,1)} %v_hbm.1, ...), custom_call_target="tpu_custom_call" | custom-call | tf_op jit(solution)/shard_map/pallas_call | solution.py:455
  28.2 1.0 %shard_map.95 = (bf16[384,1024]{1,0:T(8,128)(2,1)}, bf16[384,128]{1,0:T(8,128)(2,1)}, bf16[384,128]{1,0:T(8,128)(2,1)}) custom-call(bf16[384,1024]{1,0:T(8,128)(2,1)S(1)} %get-tuple-element.6.dq_ref, bf16[384,128]{1,0:T(8,128)(2,1)S(1)} %get-tuple-element.7.dk_ref, bf16[384,128]{1,0:T(8,128)(2,1)S(1)} %get-tuple-element.8.dv_ref), custom_call_target="tpu_custom_call" | custom-call | tf_op jit(solution)/shard_map/pallas_call | solution.py:497

commit v3 on v2

--- a/solution.py
+++ b/solution.py
@@ -77,6 +77,7 @@
     me = lax.axis_index("seq") * per_seq + lax.axis_index("rep")
     core = lax.rem(me, 2)
     partner = me + 1 - 2 * core
+    crossing = lax.rem(me, 8)
 
     def device(index):
         return (lax.div(index, per_seq), lax.rem(index, per_seq))
@@ -271,6 +272,10 @@
     def _():
         send_far.start()
 
+    @when(core == 1, crossing != 3, me + 2 < count)
+    def _():
+        send_near.start()
+
     def round_out(step):
         out[step] = acc[step].astype(jnp.bfloat16)
 
@@ -326,11 +331,11 @@
             def _():
                 sweep(kv.at[step, 0], kv.at[step, 1], full_items, acc.at[step], False)
 
-        @when(core == 1, step == 0, me + 2 < count)
+        @when(core == 1, step == 0, crossing == 3, me + 2 < count)
         def _():
             send_near.start()
 
-        @when(core == 0, step == 0, me + 4 < count)
+        @when(core == 0, step == 0, me >= 2, me + 4 < count)
         def _():
             send_far.start()
 
@@ -382,6 +387,11 @@
     @when(core == 0)
     def _():
         part_copy(1, 1).wait_recv()
+
+        @when(me < 2, me + 4 < count)
+        def _():
+            send_far.start()
+
         own_acc[...] = own_acc[...] + part[1].astype(jnp.float32)
 
     for d in (2, 4):

time: 29.4 us -> 28 us (0.952)
  Pallas kernels: 28.5 us -> 27 us
    pallas_call x1, Pallas kernels: 27.6 us -> 26 us  [shards(): pl.pallas_call(functools.partial(kernel, count, per_seq), out_shape=(jax....]
where the time goes in v3:
time: 28 us; the launch traced here: 27.6 us
  Pallas kernels  27 us (96%)
  between operations  0.64 us (2%)
    pallas_call x1, Pallas kernels, shards(): pl.pallas_call(functools.partial(kernel, count, per_seq), out_shape=(jax....  26 us
    pallas_call x1, Pallas kernels, shards(): pl.pallas_call(pass_on, out_shape=tuple((jax.ShapeDtypeStruct(x.shape, x....  0.96 us

profile of v3, /device:TPU:4, one launch (start us, length us, event | category | flops | bytes accessed | tf_op | source)
XLA Modules:
  0.0 27.6 jit_solution(1874918210638757959)
XLA Ops:
  0.6 26.0 %shard_map.94 = (bf16[384,1024]{1,0:T(8,128)(2,1)S(1)}, bf16[384,128]{1,0:T(8,128)(2,1)S(1)}, bf16[384,128]{1,0:T(8,128)(2,1)S(1)}) custom-call(s32[1,31]{1,0:T(1,128)} %bitcast.1, bf16[384,1024]{1,0:T(8,128)(2,1)} %q_hbm.1, bf16[384,1024]{1,0:T(8,128)(2,1)} %g_hbm.1, bf16[384,128]{1,0:T(8,128)(2,1)} %k_hbm.1, bf16[384,128]{1,0:T(8,128)(2,1)} %v_hbm.1, ...), custom_call_target="tpu_custom_call" | custom-call | tf_op jit(solution)/shard_map/pallas_call | solution.py:465
  26.7 1.0 %shard_map.95 = (bf16[384,1024]{1,0:T(8,128)(2,1)}, bf16[384,128]{1,0:T(8,128)(2,1)}, bf16[384,128]{1,0:T(8,128)(2,1)}) custom-call(bf16[384,1024]{1,0:T(8,128)(2,1)S(1)} %get-tuple-element.6.dq_ref, bf16[384,128]{1,0:T(8,128)(2,1)S(1)} %get-tuple-element.7.dk_ref, bf16[384,128]{1,0:T(8,128)(2,1)S(1)} %get-tuple-element.8.dv_ref), custom_call_target="tpu_custom_call" | custom-call | tf_op jit(solution)/shard_map/pallas_call | solution.py:507

commit v4 on v3

--- a/solution.py
+++ b/solution.py
@@ -137,9 +137,21 @@
     def part_copy(step, slot):
         return remote(out.at[step], part.at[slot], part_send.at[slot], part_recv.at[slot], partner)
 
-    def ret_copy(step, d):
-        n = d // 2 - 1
-        return remote(out.at[step], ret.at[n], ret_send.at[n], ret_recv.at[n], me - d)
+    parts = [(wide // tile, rows // tile), (0, wide // tile)]
+
+    def ret_copies(step, d):
+        if d == 2:
+            return [remote(out.at[step], ret.at[0], ret_send.at[0], ret_recv.at[0], me - d)]
+        return [
+            remote(
+                out.at[step, :, i:j],
+                ret.at[1, :, i:j],
+                ret_send.at[1 + n],
+                ret_recv.at[1 + n],
+                me - d,
+            )
+            for n, (i, j) in enumerate(parts)
+        ]
 
     send_partner = kv_copy(own, 0, 2, partner)
     send_near = kv_copy(own, 3 * core, 0, me + 2)
@@ -225,17 +237,17 @@
             put(dq_t, (slice(None), slice(h * rows + t, h * rows + t + n)), dq[:, at : at + n], first_dq)
             at += n
 
-    def sweep(k_ref, v_ref, items, acc_ref, first_dq, before=None):
+    def sweep(k_ref, v_ref, items, acc_ref, first_dq, before=None, depth=1):
         seen = set()
-        held = None
+        held = []
         for n, item in enumerate(items):
             if before is not None:
                 before(n)
-            ahead = scores(k_ref, v_ref, item)
-            if held is not None:
-                finish(*held, acc_ref, seen, first_dq)
-            held = (item, *ahead)
-        finish(*held, acc_ref, seen, first_dq)
+            held.append((item, *scores(k_ref, v_ref, item)))
+            if len(held) > depth:
+                finish(*held.pop(0), acc_ref, seen, first_dq)
+        for rest in held:
+            finish(*rest, acc_ref, seen, first_dq)
 
     def runs(begin, width):
         pieces = []
@@ -253,6 +265,8 @@
         ([(h, t, tile) for h in pair], 0, t + tile) for pair in pairs for t in reversed(range(0, rows, tile))
     ]
     far_items = [([(h, t, tile) for h in pair], t, rows) for pair in pairs for t in range(0, rows, tile)]
+    late_items = [(pieces, max(low, wide), rows) for pieces, low, _ in far_items]
+    early_items = [(pieces, low, wide) for pieces, low, _ in far_items if low < wide]
 
     set_bias(0)
     k_t[...] = turned(own[0])
@@ -282,7 +296,8 @@
     def merge_out(step, slot, d):
         part_copy(step, slot).wait_recv()
         out[step] = (acc[step] + part[slot].astype(jnp.float32)).astype(jnp.bfloat16)
-        ret_copy(step, d).start()
+        for copy in ret_copies(step, d):
+            copy.start()
 
     def arrive(slot):
         kv_copy(own, slot, 0, partner).wait_recv()
@@ -325,7 +340,17 @@
 
             @when(d == REACH)
             def _():
-                sweep(kv.at[step, 0], kv.at[step, 1], far_items, acc.at[step], False)
+                @when(core == 1)
+                def _():
+                    sweep(kv.at[2, 0], kv.at[2, 1], far_items, acc.at[2], False)
+
+                @when(core == 0)
+                def _():
+                    todo = zip(ret_copies(3, 4), (late_items, early_items), parts, (2, 1))
+                    for copy, items, (i, j), depth in todo:
+                        sweep(kv.at[3, 0], kv.at[3, 1], items, acc.at[3], False, depth=depth)
+                        out[3, :, i:j] = acc[3, :, i:j].astype(jnp.bfloat16)
+                        copy.start()
 
             @when(d != REACH)
             def _():
@@ -353,11 +378,6 @@
             round_out(2)
             part_copy(2, 0).start()
 
-        @when(core == 0, step == 3, me >= 4)
-        def _():
-            round_out(3)
-            ret_copy(3, 4).start()
-
         @when(core == 1, step == 0)
         def _():
             round_out(0)
@@ -398,7 +418,8 @@
 
         @when(me + d < count)
         def _():
-            ret_copy(0, d).wait_recv()
+            for copy in ret_copies(0, d):
+                copy.wait_recv()
             own_acc[...] = own_acc[...] + ret[d // 2 - 1].astype(jnp.float32)
 
     for i in range(rows // tile):
@@ -424,11 +445,13 @@
     def _():
         kv_copy(kv.at[0], 1, 3, partner).wait_send()
         part_copy(0, 0).wait_send()
-        ret_copy(0, 2).wait_send()
+        for copy in ret_copies(0, 2):
+            copy.wait_send()
 
     @when(me >= 4)
     def _():
-        ret_copy(0, 4).wait_send()
+        for copy in ret_copies(0, 4):
+            copy.wait_send()
 
     @when(core == 1, me >= 4)
     def _():
@@ -497,8 +520,8 @@
             pltpu.SemaphoreType.DMA((REACH,)),
             pltpu.SemaphoreType.DMA((2,)),
             pltpu.SemaphoreType.DMA((2,)),
-            pltpu.SemaphoreType.DMA((2,)),
-            pltpu.SemaphoreType.DMA((2,)),
+            pltpu.SemaphoreType.DMA((3,)),
+            pltpu.SemaphoreType.DMA((3,)),
         ],
         compiler_params=pltpu.CompilerParams(
             collective_id=0, has_side_effects=True, vmem_limit_bytes=40 * MIB

time: 28 us -> 27.8 us (level)
  no operation moved by 1% of the time
where the time goes in v4:
time: 27.8 us; the launch traced here: 27.6 us
  Pallas kernels  27 us (97%)
  between operations  0.64 us (2%)
    pallas_call x1, Pallas kernels, shards(): pl.pallas_call(functools.partial(kernel, count, per_seq), out_shape=(jax....  26 us
    pallas_call x1, Pallas kernels, shards(): pl.pallas_call(pass_on, out_shape=tuple((jax.ShapeDtypeStruct(x.shape, x....  0.96 us

profile of v4, /device:TPU:4, one launch (start us, length us, event | category | flops | bytes accessed | tf_op | source)
XLA Modules:
  0.0 27.6 jit_solution(9773763883688160803)
XLA Ops:
  0.6 26.0 %shard_map.94 = (bf16[384,1024]{1,0:T(8,128)(2,1)S(1)}, bf16[384,128]{1,0:T(8,128)(2,1)S(1)}, bf16[384,128]{1,0:T(8,128)(2,1)S(1)}) custom-call(s32[1,31]{1,0:T(1,128)} %bitcast.1, bf16[384,1024]{1,0:T(8,128)(2,1)} %q_hbm.1, bf16[384,1024]{1,0:T(8,128)(2,1)} %g_hbm.1, bf16[384,128]{1,0:T(8,128)(2,1)} %k_hbm.1, bf16[384,128]{1,0:T(8,128)(2,1)} %v_hbm.1, ...), custom_call_target="tpu_custom_call" | custom-call | tf_op jit(solution)/shard_map/pallas_call | solution.py:488
  26.7 1.0 %shard_map.95 = (bf16[384,1024]{1,0:T(8,128)(2,1)}, bf16[384,128]{1,0:T(8,128)(2,1)}, bf16[384,128]{1,0:T(8,128)(2,1)}) custom-call(bf16[384,1024]{1,0:T(8,128)(2,1)S(1)} %get-tuple-element.6.dq_ref, bf16[384,128]{1,0:T(8,128)(2,1)S(1)} %get-tuple-element.7.dk_ref, bf16[384,128]{1,0:T(8,128)(2,1)S(1)} %get-tuple-element.8.dv_ref), custom_call_target="tpu_custom_call" | custom-call | tf_op jit(solution)/shard_map/pallas_call | solution.py:530
